TPU v7x, 32 devices: a whole 2x2x4 slice. The times are simulated.
32 devices in a mesh: dp: 16 (over z, x, core), tensor: 2 (over y).
Axes of the slice: x: 2, y: 2, z: 4, core: 2. Of those that a mesh axis runs over, the one named last changes fastest.
Arguments:
- drafter_hidden: bfloat16 [2, 2048, 4096], P(None, 'dp', 'tensor'), may hold values from -2000 to 2000
- norm_gain: bfloat16 [4096], P('tensor'), may hold values from 0.5 to 1.5
- head_weight: bfloat16 [4096, 8192], P('tensor', 'dp'), may hold values from -24 to 24
- labels: int32 [2048], P('dp'), may hold values from 0 to 8191
- loss_mask: int32 [2048], P('dp'), may hold values 0 or 1
- offsets: int32 [2], replicated, may hold values from 1 to 4
Outputs:
- draft_loss: float32 [], replicated
- head_grad: float32 [4096, 8192], P('tensor', 'dp')
All inputs are finite; a program needn't handle non-finite values. No bound on the sum of `loss_mask` on one device may be relied on, other than what follows from the above.
Results may differ from a plain program's by a relative error of at most 0.0048.
Values may be sent and summed in bfloat16 or wider, within the bound.
A program may use at most 128 MiB of HBM per device.

v0:
```python
import functools

import jax
import jax.numpy as jnp
from jax import lax
from jax.experimental import pallas as pl
from jax.experimental.pallas import tpu as pltpu
from jax.sharding import PartitionSpec as P

WINDOW = 512
MAXOFF = 4

epsilon = 1e-05
step_decay = 0.8
MESH = pl.DeviceIdType.MESH


def spread_kernel(axes, sizes, *refs):
    count = len(axes)
    sources, targets = refs[:count], refs[count : 2 * count]
    held, sems = refs[2 * count : 3 * count], refs[3 * count :]
    barrier = pltpu.get_barrier_semaphore()
    peers = 0
    for axis, size in dict(zip(axes, sizes)).items():
        me = lax.axis_index(axis)
        for j in range(1, size):
            pl.semaphore_signal(
                barrier, inc=1, device_id={axis: lax.rem(me + j, size)}, device_id_type=MESH
            )
            peers += 1
    pl.semaphore_wait(barrier, peers)
    copies = []
    for k in range(count):
        me = lax.axis_index(axes[k])
        for j in range(1, sizes[k]):
            copy = pltpu.make_async_remote_copy(
                src_ref=sources[k],
                dst_ref=held[k].at[me],
                send_sem=sems[2 * k].at[j],
                recv_sem=sems[2 * k + 1].at[j],
                device_id={axes[k]: lax.rem(me + j, sizes[k])},
                device_id_type=MESH,
            )
            copy.start()
            copies.append(copy)
    for k in range(count):
        held[k][lax.axis_index(axes[k])] = sources[k][...]
    for copy in copies:
        copy.wait()
    for k in range(count):
        targets[k][...] = held[k][...]


def spread(pairs, identity):
    arrays = [a for a, _ in pairs]
    axes = [axis for _, axis in pairs]
    sizes = [lax.axis_size(axis) for axis in axes]
    shapes = [(size, *a.shape) for a, size in zip(arrays, sizes)]
    vmem = pl.BlockSpec(memory_space=pltpu.VMEM)
    sems = []
    for size in sizes:
        sems += [pltpu.SemaphoreType.DMA((size,))] * 2
    return pl.pallas_call(
        functools.partial(spread_kernel, axes, sizes),
        out_shape=[jax.ShapeDtypeStruct(s, a.dtype) for s, a in zip(shapes, arrays)],
        in_specs=[vmem] * len(arrays),
        out_specs=[vmem] * len(arrays),
        scratch_shapes=[pltpu.VMEM(s, a.dtype) for s, a in zip(shapes, arrays)] + sems,
        compiler_params=pltpu.CompilerParams(collective_id=identity, has_side_effects=True),
        name=f"spread{identity}",
    )(*arrays)


def logits_kernel(
    n, ways, normed, weight, *refs
):
    gathered = refs[:ways]
    logits, held, part, landed, send, recv, part_send, part_recv, out_sem, own_sem = refs[ways:]
    steps, rows, vocab = part.shape[1:]
    mine = rows // ways
    line = n // 4
    me, rank = lax.axis_index("dp"), lax.axis_index("tensor")
    c, x, z = lax.rem(me, 2), lax.rem(me // 2, 2), me // 4
    sibling, other = 1 - c, 1 - x

    def at(z_, x_, c_):
        return (z_ * 2 + x_) * 2 + c_

    own = pltpu.make_async_copy(normed, held.at[me], own_sem)
    own.start()
    barrier = pltpu.get_barrier_semaphore()

    def greet(device):
        pl.semaphore_signal(barrier, inc=1, device_id=device, device_id_type=MESH)

    @pl.when(z > 0)
    def _():
        greet({"dp": at(z - 1, x, c)})

    @pl.when(z < line - 1)
    def _():
        greet({"dp": at(z + 1, x, c)})

    greet({"dp": at(z, other, c)})
    greet({"dp": at(z, x, sibling)})
    for j in range(1, ways):
        greet({"tensor": lax.rem(rank + j, ways)})
    chips = jnp.where(z > 0, 1, 0) + jnp.where(z < line - 1, 1, 0)
    pl.semaphore_wait(barrier, chips + 1 + ways)
    own.wait()

    def block_copy(kind, b, s, target):
        return pltpu.make_async_remote_copy(
            src_ref=held.at[b, s],
            dst_ref=held.at[b, s],
            send_sem=send.at[kind, b, s],
            recv_sem=recv.at[b, s],
            device_id={"dp": target},
            device_id_type=MESH,
        )

    def ups(b, s):
        return block_copy(0, b, s, at(z + 1, x, c))

    def downs(b, s):
        return block_copy(1, b, s, at(z - 1, x, c))

    def across(b, s):
        return block_copy(2, b, s, at(z, other, c))

    def beside(b, s):
        return block_copy(3, b, s, at(z, x, sibling))

    def part_copy(j, b, s):
        peer = lax.rem(rank + j, ways)
        return pltpu.make_async_remote_copy(
            src_ref=part.at[b, s, pl.ds(pl.multiple_of(peer * mine, mine), mine)],
            dst_ref=landed.at[j - 1, b, s],
            send_sem=part_send.at[j - 1, b, s],
            recv_sem=part_recv.at[j - 1, b, s],
            device_id={"tensor": peer},
            device_id_type=MESH,
        )

    def out_copy(far, b, s):
        owner = lax.rem(rank - far + ways, ways)
        return pltpu.make_async_copy(
            held.at[b, s, pl.ds(pl.multiple_of(owner * mine, mine), mine)],
            gathered[far].at[b, s],
            out_sem.at[far, b, s],
        )

    def inside(zz):
        return jnp.logical_and(zz >= 0, zz < line)

    def stage(t, carry):
        k, s = t // steps, lax.rem(t, steps)
        for side in (0, 1):
            zz = z + k if side else z - k
            ok = jnp.logical_and(inside(zz), k > 0) if side else inside(zz)

            @pl.when(ok)
            def _(zz=zz):
                b = at(zz, x, c)

                @pl.when(k > 0)
                def _():
                    beside(b, s).wait_recv()

                @pl.when(jnp.logical_and(zz <= z, z < line - 1))
                def _():
                    ups(b, s).start()

                @pl.when(jnp.logical_and(zz >= z, z > 0))
                def _():
                    downs(b, s).start()

                across(b, s).start()
                beside(b, s).start()

        for side in (0, 1):
            zz = z + (k - 1) if side else z - (k - 1)
            ok = jnp.logical_and(inside(zz), k > side)

            @pl.when(ok)
            def _(zz=zz):
                b = at(zz, other, c)
                beside(b, s).wait_recv()
                beside(b, s).start()

        def multiply(q, carry):
            core, kind, side = q // 4, lax.rem(q // 2, 2), lax.rem(q, 2)
            away = k - kind
            zz = z + away * (2 * side - 1)
            ok = jnp.logical_and(inside(zz), away >= side)

            @pl.when(ok)
            def _():
                b = at(zz, lax.rem(x + kind, 2), lax.rem(c + core, 2))

                @pl.when(core > 0)
                def _():
                    beside(b, s).wait_recv()

                for far in range(ways):
                    out_copy(far, b, s).start()
                part[b, s] = jnp.dot(held[b, s], weight[...], preferred_element_type=jnp.float32)
                for j in range(1, ways):
                    part_copy(j, b, s).start()

            return carry

        return lax.fori_loop(0, 8, multiply, carry)

    lax.fori_loop(0, (line + 1) * steps, stage, 0)

    def finish(u, carry):
        b, s = u // steps, lax.rem(u, steps)
        cb, xb, zb = lax.rem(b, 2), lax.rem(b // 2, 2), b // 4
        column = jnp.logical_and(xb == x, cb == c)

        @pl.when(jnp.logical_and(column, jnp.logical_and(zb <= z, z < line - 1)))
        def _():
            ups(b, s).wait_send()

        @pl.when(jnp.logical_and(column, jnp.logical_and(zb >= z, z > 0)))
        def _():
            downs(b, s).wait_send()

        @pl.when(column)
        def _():
            across(b, s).wait_send()

        @pl.when(cb == c)
        def _():
            beside(b, s).wait_send()

        for far in range(ways):
            out_copy(far, b, s).wait()
        for j in range(1, ways):
            part_copy(j, b, s).wait_recv()
        total = part[b, s, pl.ds(pl.multiple_of(rank * mine, mine), mine)]
        for j in range(1, ways):
            total += landed[j - 1, b, s]
        logits[b, s] = total
        for j in range(1, ways):
            part_copy(j, b, s).wait_send()
        return carry

    lax.fori_loop(0, n * steps, finish, 0)


def gather_and_multiply(normed, weight):
    steps, rows, width = normed.shape
    vocab = weight.shape[1]
    n, ways = lax.axis_size("dp"), lax.axis_size("tensor")
    mine = rows // ways
    vmem = pl.BlockSpec(memory_space=pltpu.VMEM)
    hbm = pl.BlockSpec(memory_space=pl.ANY)
    dma = pltpu.SemaphoreType.DMA
    return pl.pallas_call(
        functools.partial(logits_kernel, n, ways),
        out_shape=[
            *[jax.ShapeDtypeStruct((n, steps, mine, width), jnp.bfloat16)] * ways,
            jax.ShapeDtypeStruct((n, steps, mine, vocab), jnp.float32),
        ],
        in_specs=[hbm, vmem],
        out_specs=[hbm] * ways + [vmem],
        scratch_shapes=[
            pltpu.VMEM((n, steps, rows, width), jnp.bfloat16),
            pltpu.VMEM((n, steps, rows, vocab), jnp.float32),
            pltpu.VMEM((ways - 1, n, steps, mine, vocab), jnp.float32),
            dma((4, n, steps)),
            dma((n, steps)),
            dma((ways - 1, n, steps)),
            dma((ways - 1, n, steps)),
            dma((ways, n, steps)),
            dma,
        ],
        compiler_params=pltpu.CompilerParams(
            collective_id=7, has_side_effects=True, vmem_limit_bytes=60 * 1024 * 1024
        ),
        name="gather_and_multiply",
    )(normed, weight)


def local(drafter_hidden, norm_gain, head_weight, labels, loss_mask, offsets):
    step_count, local_tokens, width_part = drafter_hidden.shape
    vocab_part = head_weight.shape[1]
    data_ways = lax.axis_size("dp")
    tensor_ways = lax.axis_size("tensor")
    data_rank = lax.axis_index("dp")
    tensor_rank = lax.axis_index("tensor")
    all_tokens = local_tokens * data_ways
    rows_each = local_tokens // tensor_ways
    hidden_wide = drafter_hidden.astype(jnp.float32)
    squares_all, token_all = spread(
        [
            (jnp.sum(hidden_wide * hidden_wide, axis=-1), "tensor"),
            (jnp.stack([labels, loss_mask]), "dp"),
        ],
        5,
    )
    inverse = lax.rsqrt(jnp.sum(squares_all, axis=0) / (width_part * tensor_ways) + epsilon)
    normed = (hidden_wide * inverse[:, :, None] * norm_gain.astype(jnp.float32)).astype(
        jnp.bfloat16
    )
    *gathered, logits = gather_and_multiply(normed, head_weight)

    everywhere = jnp.arange(all_tokens, dtype=jnp.int32)

    def moved(values, by):
        padded = jnp.concatenate([values, jnp.broadcast_to(values[-1:], (MAXOFF,))])
        result = padded[MAXOFF : MAXOFF + all_tokens]
        for far in range(1, MAXOFF):
            result = jnp.where(by == far, padded[far : far + all_tokens], result)
        return result

    def own_rows(values):
        grid = values.reshape(data_ways, local_tokens)
        return lax.dynamic_slice_in_dim(grid, tensor_rank * rows_each, rows_each, 1)

    label_flat = token_all[:, 0].reshape(all_tokens)
    mask_flat = token_all[:, 1].reshape(all_tokens)
    label_list, weight_list, count_list = [], [], []
    for step_at in range(step_count):
        by = offsets[step_at]
        inside = everywhere % WINDOW + by < WINDOW
        weights = jnp.where(inside, moved(mask_flat, by), 0).astype(jnp.float32)
        count_list.append(jnp.sum(weights))
        weight_list.append(own_rows(weights))
        label_list.append(own_rows(moved(label_flat, by)))
    row_label = jnp.stack(label_list, axis=1)
    row_weight = jnp.stack(weight_list, axis=1)
    counted = jnp.stack(count_list)
    factors = step_decay ** jnp.arange(step_count, dtype=jnp.float32)

    columns = data_rank * vocab_part + jnp.arange(vocab_part, dtype=jnp.int32)
    hitting = columns == row_label[..., None]
    local_top = jnp.max(logits, axis=-1)
    label_part = jnp.sum(jnp.where(hitting, logits, 0.0), axis=-1)
    local_lse = local_top + jnp.log(jnp.sum(jnp.exp(logits - local_top[..., None]), axis=-1))
    label_sum = jnp.sum(row_weight * label_part, axis=(0, 2))
    lse_rows = local_lse.reshape(-1, local_tokens)
    label_rows = jnp.broadcast_to(label_sum[:, None], (step_count, local_tokens))
    (spread_all,) = spread([(jnp.concatenate([lse_rows, label_rows]), "dp")], 6)
    lse_all = spread_all[:, : lse_rows.shape[0]]
    label_total = jnp.sum(spread_all[:, lse_rows.shape[0] :, 0], axis=0)
    top = jnp.max(lse_all, axis=0)
    log_total = (top + jnp.log(jnp.sum(jnp.exp(lse_all - top), axis=0))).reshape(local_lse.shape)
    softmax = jnp.exp(logits - log_total[..., None])
    slopes = (
        factors[:, None, None] * row_weight[..., None] * (softmax - hitting.astype(jnp.float32))
    ).astype(jnp.bfloat16)

    parts = [slopes]
    for far in range(1, tensor_ways):
        parts.append(
            lax.ppermute(
                slopes, "tensor", [(i, (i + far) % tensor_ways) for i in range(tensor_ways)]
            )
        )
    gradient = sum(
        jnp.einsum("nsrd,nsrv->dv", rows, part, preferred_element_type=jnp.float32)
        for rows, part in zip(gathered, parts)
    )

    own_sum = jnp.sum(row_weight * log_total, axis=(0, 2)) - label_total
    (sums_all,) = spread(
        [(jnp.broadcast_to(own_sum[:, None], (step_count, local_tokens)), "tensor")], 8
    )
    numerator = jnp.sum(sums_all[:, :, 0], axis=0)
    loss_total = jnp.sum(factors * numerator / counted)
    return (loss_total, gradient)


def solution(mesh):
    return jax.shard_map(
        local,
        mesh=mesh,
        in_specs=(P(None, "dp", "tensor"), P("tensor"), P("tensor", "dp"), P("dp"), P("dp"), P()),
        out_specs=(P(), P("tensor", "dp")),
        check_vma=False,
    )
```

profile of v0, /device:TPU:0, one launch (start us, length us, event | category | flops | bytes accessed | tf_op | source)
XLA Modules:
  0.0 228.3 jit_solution(12554543558364483176)
XLA Ops:
  0.6 1.3 fusion.15
  5.8 2.1 fusion.4.refs_0_
  7.9 1.2 pad_add_fusion.1.refs_1_
  9.1 10.7 %spread5.1 = (f32[2,2,128]{2,1,0:T(2,128)}, s32[16,2,128]{2,1,0:T(2,128)}) custom-call(f32[2,128]{1,0:T(2,128)} %fusion.4.refs_0_, s32[2,128]{1,0:T(2,128)} %pad_add_fusion.1.refs_1_), custom_call_target="tpu_custom_call" | custom-call | tf_op jit(solution)/shard_map/spread5/pallas_call | solution.py:63
  19.8 0.8 fusion.14
  20.6 0.6 slice.78
  21.2 0.7 slice.79
  21.9 2.7 %convert_reduce_fusion.1 = (f32[]{:T(128)}, s32[2048]{0:T(1024)S(1)}, f32[]{:T(128)}, s32[2048]{0:T(1024)S(1)}) fusion(s32[]{:T(128)} %bitcast, pred[]{:T(512)S(6)} %eq.42, pred[]{:T(512)S(6)} %eq.41, s32[2048]{0:T(1024)S(1)} %bitcast.49, s32[]{:T(128)} %bitcast.4, pred[]{:T(512)S(6)} %eq.40, pred[]{:T(512)S(6)} %eq.45, pred[]{:T(512)S(6)} %eq.44, ...), kind=kLoop, calls=%fused_computation.42 | loop fusion | flops 45054 | bytes 24602 | tf_op jit(solution)/shard_map/reduce_sum | solution.py:330
  24.6 0.8 select_bitcast_fusion.1
  25.3 0.7 convert_element_type.30
  26.0 0.7 reduce_sum.109
  26.7 2.5 %fusion.6.normed = bf16[2,128,2048]{2,1,0:T(8,128)(2,1)} fusion(bf16[2,128,2048]{2,1,0:T(8,128)(2,1)} %param.6, f32[2048]{0:T(1024)S(1)} %convert_element_type.30, f32[2,128]{1,0:T(2,128)S(1)} %add_rsqrt_fusion), kind=kLoop, calls=%fused_computation.12 | loop fusion | flops 2097152 | bytes 2106368 | tf_op jit(solution)/shard_map/convert_element_type | solution.py:305
  29.2 106.6 %gather_and_multiply.1 = (bf16[16,2,64,2048]{3,2,1,0:T(8,128)(2,1)}, bf16[16,2,64,2048]{3,2,1,0:T(8,128)(2,1)}, f32[16,2,64,512]{3,2,1,0:T(8,128)}) custom-call(bf16[2,128,2048]{2,1,0:T(8,128)(2,1)} %fusion.6.normed, bf16[2048,512]{1,0:T(8,128)(2,1)} %weight.1), custom_call_target="tpu_custom_call" | custom-call | tf_op jit(solution)/shard_map/gather_and_multiply/pallas_call | solution.py:261
  135.8 2.5 %reduce_max.18 = f32[16,2,64]{2,1,0:T(2,128)S(1)} reduce(f32[16,2,64,512]{3,2,1,0:T(8,128)} %get-tuple-element.9, f32[]{:T(128)} %constant.52.clone.1), dimensions={3}, to_apply=%region_2.3 | reduce | flops 1046528 | bytes 4202500 | tf_op jit(solution)/shard_map/reduce_max | solution.py:340
  138.5 1.3 fusion.9
  139.8 3.2 %fusion = (f32[16,2,64]{2,1,0:T(2,128)S(1)}, f32[16,2,64]{2,1,0:T(2,128)S(1)}) fusion(f32[16,2,64,512]{3,2,1,0:T(8,128)} %get-tuple-element.9, s32[16,2,64]{2,1,0:T(2,128)S(1)} %pad_add_fusion, s32[512]{0:T(512)S(1)} %iota_add_fusion, f32[16,2,64]{2,1,0:T(2,128)S(1)} %reduce_max.18), kind=kLoop, calls=%fused_computation.2 | loop fusion | flops 5238784 | bytes 4229120 | tf_op jit(solution)/shard_map/reduce_sum | solution.py:341
  143.1 0.1 add.104
  143.2 0.1 multiply_reduce_fusion.1
  143.4 0.7 pad_maximum_fusion.1.refs_0_
  144.1 10.3 %spread6.1 = f32[16,18,128]{2,1,0:T(8,128)} custom-call(f32[18,128]{1,0:T(8,128)} %pad_maximum_fusion.1.refs_0_), custom_call_target="tpu_custom_call" | custom-call | tf_op jit(solution)/shard_map/spread6/pallas_call | solution.py:63
  154.4 0.9 slice_reduce_fusion
  155.3 0.9 exponential_reduce_fusion.1
  156.3 0.1 broadcast_multiply_fusion
  156.5 2.9 %fusion.3 = bf16[16,2,64,512]{3,2,1,0:T(8,128)(2,1)S(1)} fusion(f32[16,2,64,512]{3,2,1,0:T(8,128)} %get-tuple-element.9, f32[16,2,64]{2,1,0:T(2,128)S(1)} %add.108, f32[16,2,64]{2,1,0:T(2,128)S(1)} %get-tuple-element.18, s32[16,2,64]{2,1,0:T(2,128)S(1)} %pad_add_fusion, s32[512]{0:T(512)S(1)} %iota_add_fusion), kind=kLoop, calls=%fused_computation.5 | loop fusion | flops 6291456 | bytes 6318080 | tf_op jit(solution)/shard_map/convert_element_type | solution.py:354
  159.3 0.3 collective-permute-start
  159.7 1.0 slice_reduce_fusion.1
  160.7 0.6 broadcast_in_dim.18.refs_0_
  161.3 46.7 %spread8.1 = f32[2,2,128]{2,1,0:T(2,128)} custom-call(f32[2,128]{1,0:T(2,128)} %broadcast_in_dim.18.refs_0_), custom_call_target="tpu_custom_call" | custom-call | tf_op jit(solution)/shard_map/spread8/pallas_call | solution.py:63
  208.0 0.8 slice_reduce_fusion.2
  208.8 2.0 fusion.13
  210.8 6.9 %fusion.16 = f32[2048,512,1,1]{1,0,3,2:T(8,128)S(1)} fusion(bf16[16,2,64,2048]{3,2,1,0:T(8,128)(2,1)} %get-tuple-element.10, bf16[16,2,64,512]{3,2,1,0:T(8,128)(2,1)S(1)} %fusion.3), kind=kOutput, calls=%fused_computation.66 | convolution fusion | flops 4294967296 | bytes 14680064 | tf_op jit(solution)/shard_map/nsrd,nsrv->dv/dot_general | solution.py:364
  217.8 10.6 %bitcast_add_fusion = f32[2048,512]{1,0:T(8,128)} fusion(f32[2048,512,1,1]{1,0,3,2:T(8,128)S(1)} %fusion.16, bf16[16,2,64,2048]{3,2,1,0:T(8,128)(2,1)} %get-tuple-element.11, bf16[16,2,64,512]{3,2,1,0:T(8,128)(2,1)} %collective-permute-done), kind=kOutput, calls=%fused_computation.6 | convolution fusion | flops 4296015872 | bytes 18874368 | tf_op jit(solution)/shard_map/nsrd,nsrv->dv/dot_general | solution.py:364
  (12 shorter events, 0.3 us)
Async XLA Ops:
  159.3 58.4 %collective-permute-start = (bf16[16,2,64,512]{3,2,1,0:T(8,128)(2,1)S(1)}, bf16[16,2,64,512]{3,2,1,0:T(8,128)(2,1)}, u32[]{:S(2)}, u32[]{:S(2)}) collective-permute-start(bf16[16,2,64,512]{3,2,1,0:T(8,128)(2,1)S(1)} %fusion.3), channel_id=1, source_target_pairs={{0,1},{1,0},{2,3},{3,2},{4,5},{5,4},{6,7},{7,6},{8,9},{9,8},{10,11... | collective-permute-start | bytes 6291464 | tf_op jit(solution)/shard_map/ppermute | solution.py:359
where the time goes:
time: 229 us; the launch traced here: 228 us
  Pallas kernels  174 us (76%)
  other arithmetic  27.3 us (12%)
  matrix products  17.5 us (8%)
  between operations  4.54 us (2%)
  local copies, waits for them, and re-layouts  4.36 us (2%)
    pallas_call x1, Pallas kernels, gather_and_multiply(): pl.pallas_call(functools.partial(logits_kernel, n, ways), out_shape=[*[ja...  107 us
    pallas_call x3, Pallas kernels, spread(): pl.pallas_call(functools.partial(spread_kernel, axes, sizes), out_shape=[...  67.7 us
    dot_general x2, matrix products, local(): jnp.einsum('nsrd,nsrv->dv', rows, part, preferred_element_type=jnp.float32)  17.5 us
  transfers between devices with their start and end apart: 1, of which 0 were waited for; matrix products, arithmetic and copies ran while one was open for 5% of the time, Pallas kernels for 20%

commit v1 on v0

v1 whole, which is shorter than its diff:
```python
import functools

import jax
import jax.numpy as jnp
from jax import lax
from jax.experimental import pallas as pl
from jax.experimental.pallas import tpu as pltpu
from jax.sharding import PartitionSpec as P

WINDOW = 512
MAXOFF = 4
LANES = 128

epsilon = 1e-05
step_decay = 0.8
MESH = pl.DeviceIdType.MESH

PACE = 2
LAG = 1
EARLY = 3


def rows_to_columns(row):
    return jnp.transpose(jnp.broadcast_to(row, (LANES, row.shape[1])))


def head_kernel(
    n, ways, x_in, gain, w_in, labels, mask, offsets, grad, loss,
    xv, held, wall, logits, s_own, s_got, labcol, wcol, lcol, tok, statall, lserow, labpart, num,
    count, sqall, invcol, lossall,
    send, recv, xsend, wsend, wrecv, sqsend, sqrecv, ssend, srecv, tsend, trecv, gsend, grecv,
    lsend, lrecv, local_sem,
):
    steps, rows, width = xv.shape
    vocab = w_in.shape[1]
    pieces = held.shape[0]
    each = rows // ways
    line = n // 4
    total_rows = n * each
    groups = total_rows // LANES
    main = steps * ways
    per_step = PACE * ways
    me, rank = lax.axis_index("dp"), lax.axis_index("tensor")
    c, x, z = lax.rem(me, 2), lax.rem(me // 2, 2), me // 4
    sibling, other = 1 - c, 1 - x
    f32 = jnp.float32

    def at(z_, x_, c_):
        return (z_ * 2 + x_) * 2 + c_

    def second(q, far):
        return main + q * (ways - 1) + far - 1

    x_load = pltpu.make_async_copy(x_in, xv, local_sem.at[0])
    x_load.start()
    w_load = pltpu.make_async_copy(w_in, wall.at[0], local_sem.at[1])
    w_load.start()

    barrier = pltpu.get_barrier_semaphore()
    for j in range(1, n):
        pl.semaphore_signal(
            barrier, inc=1, device_id={"dp": lax.rem(me + j, n)}, device_id_type=MESH
        )
    for j in range(1, ways):
        pl.semaphore_signal(
            barrier, inc=1, device_id={"tensor": lax.rem(rank + j, ways)}, device_id_type=MESH
        )

    def to_tensor(src, dst, send_sem, recv_sem, far):
        return pltpu.make_async_remote_copy(
            src_ref=src,
            dst_ref=dst,
            send_sem=send_sem,
            recv_sem=recv_sem,
            device_id={"tensor": lax.rem(rank + far, ways)},
            device_id_type=MESH,
        )

    def to_dp(src, dst, send_sem, recv_sem, target):
        return pltpu.make_async_remote_copy(
            src_ref=src,
            dst_ref=dst,
            send_sem=send_sem,
            recv_sem=recv_sem,
            device_id={"dp": target},
            device_id_type=MESH,
        )

    def square_copy(far):
        return to_tensor(
            sqall.at[0], sqall.at[ways - far], sqsend.at[far - 1], sqrecv.at[ways - far - 1], far
        )

    def w_copy(far):
        return to_tensor(
            w_in, wall.at[ways - far], wsend.at[far - 1], wrecv.at[ways - far - 1], far
        )

    def x_copy(q, far):
        target = q * ways + ways - far
        return to_tensor(
            held.at[second(q, far), me],
            held.at[target, me],
            xsend.at[q, far - 1],
            recv.at[target, me],
            far,
        )

    def slope_copy(q, far):
        return to_tensor(
            s_own.at[q],
            s_got.at[ways - far - 1, q],
            gsend.at[far - 1, q],
            grecv.at[ways - far - 1, q],
            far,
        )

    def loss_copy(far):
        return to_tensor(
            lossall.at[0], lossall.at[ways - far], lsend.at[far - 1], lrecv.at[ways - far - 1], far
        )

    def token_copy(j):
        target = lax.rem(me + j, n)
        return to_dp(tok.at[me], tok.at[me], tsend.at[j], trecv.at[me], target)

    def token_wait(j):
        source = lax.rem(me + j, n)
        return to_dp(tok.at[source], tok.at[source], tsend.at[j], trecv.at[source], source)

    def stat_copy(q, j):
        target = lax.rem(me + j, n)
        return to_dp(
            statall.at[q, me], statall.at[q, me], ssend.at[q, j], srecv.at[q, me], target
        )

    def stat_wait(q, j):
        source = lax.rem(me + j, n)
        return to_dp(
            statall.at[q, source], statall.at[q, source], ssend.at[q, j], srecv.at[q, source], source
        )

    def block_copy(kind, i, b, target):
        return to_dp(held.at[i, b], held.at[i, b], send.at[kind, i, b // 2], recv.at[i, b], target)

    def ups(i, b):
        return block_copy(0, i, b, at(z + 1, x, c))

    def downs(i, b):
        return block_copy(1, i, b, at(z - 1, x, c))

    def across(i, b):
        return block_copy(2, i, b, at(z, other, c))

    def beside(i, b):
        return block_copy(3, i, b, at(z, x, sibling))

    def inside(zz):
        return jnp.logical_and(zz >= 0, zz < line)

    top_half = lax.broadcasted_iota(jnp.int32, (8, rows), 0) < 4
    tok[me] = jnp.where(
        top_half,
        jnp.broadcast_to(labels[...], (8, rows)),
        jnp.broadcast_to(mask[...], (8, rows)),
    )
    x_load.wait()
    for s in range(steps):

        def square(j, acc):
            part = xv[s, :, pl.ds(pl.multiple_of(j * LANES, LANES), LANES)].astype(f32)
            return acc + part * part

        acc = lax.fori_loop(0, width // LANES, square, jnp.zeros((rows, LANES), f32))
        column = jnp.sum(acc, axis=1, keepdims=True)
        flat = jnp.transpose(jnp.broadcast_to(column, (rows, LANES)))
        sqall[0, s] = flat[0:8]

    peers = n - 1 + ways - 1
    pl.semaphore_wait(barrier, peers)
    for far in range(1, ways):
        square_copy(far).start()
    for j in range(1, n):
        token_copy(j).start()
    labpart[...] = jnp.zeros_like(labpart)
    num[...] = jnp.zeros_like(num)
    count[...] = jnp.zeros_like(count)
    statall[:, me] = jnp.zeros((steps, 2, 8, LANES), f32)
    for far in range(1, ways):
        square_copy(far).wait_recv()
    for s in range(steps):
        total = sqall[0, s]
        for p in range(1, ways):
            total = total + sqall[p, s]
        inverse = lax.rsqrt(total / (width * ways) + epsilon)
        invcol[s] = rows_to_columns(inverse[0:1])

    for s in range(steps):
        for far in range(ways):
            owner = lax.rem(rank + far, ways)
            offset = pl.multiple_of(owner * each, each)
            i = second(s, far) if far else s * ways
            scale = invcol[s, pl.ds(offset, each)]

            def normalise(j, carry, s=s, i=i, offset=offset, scale=scale):
                at_lane = pl.ds(pl.multiple_of(j * LANES, LANES), LANES)
                wide = xv[s, pl.ds(offset, each), at_lane].astype(f32)
                held[i, me, :, at_lane] = (wide * scale * gain[:, at_lane].astype(f32)).astype(
                    jnp.bfloat16
                )
                return carry

            lax.fori_loop(0, width // LANES, normalise, 0)
    for s in range(steps):
        for far in range(1, ways):
            x_copy(s, far).start()
    for far in range(1, ways):
        w_copy(far).start()

    def relay(i, k):
        valid = jnp.logical_and(jnp.logical_and(i >= 0, i < pieces), k <= line)
        early = lax.rem(i, 6) == EARLY
        foreign = jnp.logical_and(i < main, lax.rem(i, ways) > 0)

        def along(zz, b):
            @pl.when(jnp.logical_and(zz <= z, z < line - 1))
            def _():
                ups(i, b).start()

            @pl.when(jnp.logical_and(zz >= z, z > 0))
            def _():
                downs(i, b).start()

        for side in (0, 1):
            zz = z + k if side else z - k
            ok = jnp.logical_and(inside(zz), k >= side)

            @pl.when(jnp.logical_and(valid, ok))
            def _(zz=zz):
                b = at(zz, x, c)

                @pl.when(jnp.logical_or(k > 0, foreign))
                def _():
                    beside(i, b).wait_recv()

                along(zz, b)

                @pl.when(jnp.logical_or(k == 0, jnp.logical_not(early)))
                def _():
                    across(i, b).start()

                beside(i, b).start()

        for side in (0, 1):
            zz = z + (k - 1) if side else z - (k - 1)
            ok = jnp.logical_and(inside(zz), k > side)

            @pl.when(jnp.logical_and(valid, ok))
            def _(zz=zz):
                b = at(zz, other, c)
                beside(i, b).wait_recv()

                @pl.when(early)
                def _():
                    along(zz, b)

                beside(i, b).start()

    def token_block(b):
        here = tok[b].astype(f32)
        following = tok[jnp.minimum(b + 1, n - 1)].astype(f32)
        last = jnp.broadcast_to(here[:, rows - 1 : rows], (8, rows))
        following = jnp.where(b == n - 1, last, following)
        lane = lax.broadcasted_iota(jnp.int32, (8, rows), 1)
        position = lax.rem(b * rows + lane, WINDOW)
        for s in range(steps):
            by = offsets[s]
            chosen = here
            for far in range(1, MAXOFF + 1):
                shifted = jnp.where(
                    lane < rows - far,
                    pltpu.roll(here, rows - far, 1),
                    pltpu.roll(following, rows - far, 1),
                )
                chosen = jnp.where(by == far, shifted, chosen)
            weight = jnp.where(position + by < WINDOW, chosen, 0.0)[4:5]
            count[s, 0:1] = count[s, 0:1] + weight
            span = pl.ds(pl.multiple_of(b * rows, rows), rows)
            labcol[s, span] = rows_to_columns(chosen[0:1])
            wcol[s, span] = rows_to_columns(weight)

    def own_span(b):
        return pl.ds(pl.multiple_of(b * rows + rank * each, each), each)

    def hits(s, b, chunk):
        columns = (
            me * vocab + chunk * LANES + lax.broadcasted_iota(jnp.int32, (each, LANES), 1)
        ).astype(f32)
        return labcol[s, own_span(b)] == columns

    def folded(values):
        return jnp.sum(values.reshape(each // 8, 8, LANES), axis=0)

    def logits_unit(q, zz):
        for core_x in range(2):
            for p in range(ways):
                b = at(zz, core_x, sibling)
                beside(q * ways + p, b).wait_recv()
        acc = None
        for p in range(ways):
            lhs = held[q * ways + p, pl.ds(4 * zz, 4)].reshape(4 * each, width)
            part = jnp.dot(lhs, wall[p], preferred_element_type=f32)
            acc = part if acc is None else acc + part
        span = pl.ds(pl.multiple_of(zz * 4 * each, 4 * each), 4 * each)
        logits[q, span] = acc

        def block_stats(j, carry):
            b = 4 * zz + j
            span = pl.ds(pl.multiple_of(b * each, each), each)
            tile = logits[q, span]
            top = jnp.max(tile, axis=1, keepdims=True)
            lse = top + jnp.log(jnp.sum(jnp.exp(tile - top), axis=1, keepdims=True))
            lcol[q, span] = jnp.broadcast_to(lse, (each, LANES))
            found = jnp.zeros((each, LANES), f32)
            for chunk in range(vocab // LANES):
                part = tile[:, chunk * LANES : (chunk + 1) * LANES]
                found = found + jnp.where(hits(q, b, chunk), part, 0.0)
            labpart[q] = labpart[q] + folded(wcol[q, own_span(b)] * found)
            return carry

        lax.fori_loop(0, 4, block_stats, 0)

    def send_stats(q):
        def group(g, carry):
            tile = lcol[q, pl.ds(pl.multiple_of(g * LANES, LANES), LANES)]
            statall[q, me, 0, pl.ds(g, 1)] = jnp.transpose(tile)[0:1]
            return carry

        lax.fori_loop(0, groups, group, 0)
        statall[q, me, 1] = labpart[q]
        for j in range(1, n):
            stat_copy(q, j).start()

    def make_slopes(q):
        for j in range(1, n):
            stat_wait(q, j).wait_recv()

        def highest(j, top):
            return jnp.maximum(top, statall[q, j, 0])

        top = lax.fori_loop(1, n, highest, statall[q, 0, 0])

        def sums(j, carry):
            total, found = carry
            return total + jnp.exp(statall[q, j, 0] - top), found + statall[q, j, 1]

        zero = jnp.zeros((8, LANES), f32)
        total, found = lax.fori_loop(0, n, sums, (zero, zero))
        lserow[q] = top + jnp.log(total)

        def group(g, carry):
            span = pl.ds(pl.multiple_of(g * LANES, LANES), LANES)
            lcol[q, span] = rows_to_columns(lserow[q, pl.ds(g, 1)])
            return carry

        lax.fori_loop(0, groups, group, 0)
        factor = jnp.float32(1.0)
        for s in range(1, steps):
            factor = jnp.where(q == s, jnp.float32(step_decay**s), factor)

        def block(b, carry):
            span = pl.ds(pl.multiple_of(b * each, each), each)
            lse = lcol[q, span]
            weight = wcol[q, own_span(b)]
            scale = factor * weight
            for chunk in range(vocab // LANES):
                lanes = pl.ds(chunk * LANES, LANES)
                softmax = jnp.exp(logits[q, span, lanes] - lse)
                hit = jnp.where(hits(q, b, chunk), 1.0, 0.0)
                s_own[q, span, lanes] = (scale * (softmax - hit)).astype(jnp.bfloat16)
            return carry + folded(weight * lse)

        weighted = lax.fori_loop(0, n, block, zero)
        for far in range(1, ways):
            slope_copy(q, far).start()
        numerator = jnp.sum(weighted, axis=0, keepdims=True) - jnp.sum(
            jnp.sum(found, axis=0, keepdims=True), axis=1, keepdims=True
        )
        num[q] = jnp.broadcast_to(numerator, (8, LANES))

    def add_gradient(i, slopes, first):
        block = 256 if width % 256 == 0 else LANES

        def part(j, carry):
            lanes = pl.ds(pl.multiple_of(j * block, block), block)
            lhs = held[i, :, :, lanes].reshape(total_rows, block)
            value = lax.dot_general(
                lhs, slopes[...], (((0,), (0,)), ((), ())), preferred_element_type=f32
            )

            @pl.when(first)
            def _():
                grad[lanes, :] = value

            @pl.when(jnp.logical_not(first))
            def _():
                grad[lanes, :] = grad[lanes, :] + value

            return carry

        lax.fori_loop(0, width // block, part, 0)

    base = PACE * (ways - 1) + 2
    slopes_base = base + line - 1 + LAG
    got_base = PACE * (main + ways - 2) + line + 1
    got_pace = PACE * (ways - 1)
    depth = line // PACE + 1

    def wave(w, carry):
        for d in range(depth - 1, -1, -1):
            i = w // PACE - d
            relay(i, w - PACE * i)

        @pl.when(jnp.logical_and(w >= 1, w <= line))
        def _():
            @pl.when(w == 1)
            def _():
                for j in range(1, n):
                    token_wait(j).wait_recv()

            def one(j, carry):
                token_block(4 * (w - 1) + j)
                return carry

            lax.fori_loop(0, 4, one, 0)

        @pl.when(w == base)
        def _():
            w_load.wait()
            for far in range(1, ways):
                w_copy(far).wait_recv()

        t = w - base
        q, u = t // per_step, lax.rem(t, per_step)
        active = jnp.logical_and(t >= 0, jnp.logical_and(q < steps, u < line))

        @pl.when(active)
        def _():
            def one(side, carry):
                zz = z + u * (2 * side - 1)

                @pl.when(jnp.logical_and(inside(zz), u >= side))
                def _():
                    logits_unit(q, zz)

                return carry

            lax.fori_loop(0, 2, one, 0)

            @pl.when(u == line - 1)
            def _():
                send_stats(q)

        ts = w - slopes_base
        qs = ts // per_step

        @pl.when(jnp.logical_and(jnp.logical_and(ts >= 0, lax.rem(ts, per_step) == 0), qs < steps))
        def _():
            make_slopes(qs)

            @pl.when(qs == steps - 1)
            def _():
                lossall[0] = num[...]
                for far in range(1, ways):
                    loss_copy(far).start()

            add_gradient(qs * ways, s_own.at[qs], qs == 0)

        tg = w - got_base
        qg = tg // got_pace

        @pl.when(jnp.logical_and(jnp.logical_and(tg >= 0, lax.rem(tg, got_pace) == 0), qg < steps))
        def _():
            for far in range(1, ways):
                i = second(qg, far)
                slope_copy(qg, ways - far).wait_recv()

                def arrived(j, carry, i=i):
                    beside(i, 2 * j + sibling).wait_recv()
                    return carry

                lax.fori_loop(0, 2 * line, arrived, 0)
                add_gradient(i, s_got.at[far - 1, qg], False)

        return carry

    waves = max(
        PACE * (pieces - 1) + line + 1,
        slopes_base + (steps - 1) * per_step + 1,
        got_base + (steps - 1) * got_pace + 1,
    )
    lax.fori_loop(0, waves, wave, 0)

    for far in range(1, ways):
        loss_copy(far).wait_recv()
    result = jnp.zeros((8, LANES), f32)
    for s in range(steps):
        numerator = lossall[0, s]
        for p in range(1, ways):
            numerator = numerator + lossall[p, s]
        counted = jnp.sum(
            jnp.sum(count[s], axis=0, keepdims=True), axis=1, keepdims=True
        )
        result = result + step_decay**s * numerator / jnp.broadcast_to(counted, (8, LANES))
    loss[...] = result

    def finish(u, carry):
        i, b = u // n, lax.rem(u, n)
        early = lax.rem(i, 6) == EARLY
        cb, xb, zb = lax.rem(b, 2), lax.rem(b // 2, 2), b // 4
        mine = cb == c
        column = jnp.logical_and(mine, xb == x)
        lined = jnp.logical_and(mine, jnp.logical_or(xb == x, early))

        @pl.when(jnp.logical_and(lined, jnp.logical_and(zb <= z, z < line - 1)))
        def _():
            ups(i, b).wait_send()

        @pl.when(jnp.logical_and(lined, jnp.logical_and(zb >= z, z > 0)))
        def _():
            downs(i, b).wait_send()

        @pl.when(jnp.logical_and(column, jnp.logical_or(zb == z, jnp.logical_not(early))))
        def _():
            across(i, b).wait_send()

        @pl.when(mine)
        def _():
            beside(i, b).wait_send()

        return carry

    lax.fori_loop(0, pieces * n, finish, 0)
    for j in range(1, n):
        token_copy(j).wait_send()
    for far in range(1, ways):
        square_copy(far).wait_send()
        w_copy(far).wait_send()
        loss_copy(far).wait_send()
    for s in range(steps):
        for j in range(1, n):
            stat_copy(s, j).wait_send()
        for far in range(1, ways):
            x_copy(s, far).wait_send()
            slope_copy(s, far).wait_send()


def head_step(hidden, gain, weight, labels, mask, offsets):
    steps, rows, width = hidden.shape
    vocab = weight.shape[1]
    n, ways = lax.axis_size("dp"), lax.axis_size("tensor")
    each = rows // ways
    total_rows = n * each
    pieces = steps * (2 * ways - 1)
    vmem = pl.BlockSpec(memory_space=pltpu.VMEM)
    smem = pl.BlockSpec(memory_space=pltpu.SMEM)
    hbm = pl.BlockSpec(memory_space=pl.ANY)
    dma = pltpu.SemaphoreType.DMA
    f32, bf16 = jnp.float32, jnp.bfloat16
    return pl.pallas_call(
        functools.partial(head_kernel, n, ways),
        out_shape=[
            jax.ShapeDtypeStruct((width, vocab), f32),
            jax.ShapeDtypeStruct((8, LANES), f32),
        ],
        in_specs=[hbm, vmem, hbm, vmem, vmem, smem],
        out_specs=[vmem, vmem],
        scratch_shapes=[
            pltpu.VMEM((steps, rows, width), bf16),
            pltpu.VMEM((pieces, n, each, width), bf16),
            pltpu.VMEM((ways, width, vocab), bf16),
            pltpu.VMEM((steps, total_rows, vocab), f32),
            pltpu.VMEM((steps, total_rows, vocab), bf16),
            pltpu.VMEM((ways - 1, steps, total_rows, vocab), bf16),
            pltpu.VMEM((steps, n * rows, LANES), f32),
            pltpu.VMEM((steps, n * rows, LANES), f32),
            pltpu.VMEM((steps, total_rows, LANES), f32),
            pltpu.VMEM((n, 8, rows), jnp.int32),
            pltpu.VMEM((steps, n, 2, 8, LANES), f32),
            pltpu.VMEM((steps, 8, LANES), f32),
            pltpu.VMEM((steps, 8, LANES), f32),
            pltpu.VMEM((steps, 8, LANES), f32),
            pltpu.VMEM((steps, 8, rows), f32),
            pltpu.VMEM((ways, steps, 8, rows), f32),
            pltpu.VMEM((steps, rows, LANES), f32),
            pltpu.VMEM((ways, steps, 8, LANES), f32),
            dma((4, pieces, n // 2)),
            dma((pieces, n)),
            dma((steps, ways - 1)),
            dma((ways - 1,)),
            dma((ways - 1,)),
            dma((ways - 1,)),
            dma((ways - 1,)),
            dma((steps, n)),
            dma((steps, n)),
            dma((n,)),
            dma((n,)),
            dma((ways - 1, steps)),
            dma((ways - 1, steps)),
            dma((ways - 1,)),
            dma((ways - 1,)),
            dma((2,)),
        ],
        compiler_params=pltpu.CompilerParams(
            collective_id=7, has_side_effects=True, vmem_limit_bytes=60 * 1024 * 1024
        ),
        name="head_step",
    )(hidden, gain, weight, labels, mask, offsets)


def local(drafter_hidden, norm_gain, head_weight, labels, loss_mask, offsets):
    gradient, loss = head_step(
        drafter_hidden, norm_gain[None], head_weight, labels[None], loss_mask[None], offsets
    )
    return (loss[0, 0], gradient)


def solution(mesh):
    return jax.shard_map(
        local,
        mesh=mesh,
        in_specs=(P(None, "dp", "tensor"), P("tensor"), P("tensor", "dp"), P("dp"), P("dp"), P()),
        out_specs=(P(), P("tensor", "dp")),
        check_vma=False,
    )
```

time: 229 us -> 205 us (0.90)
  other arithmetic: 27.3 us -> 0 us
  Pallas kernels: 174 us -> 197 us
  matrix products: 17.5 us -> 0 us
  between operations: 4.54 us -> 0.64 us
  local copies, waits for them, and re-layouts: 4.36 us -> 7.12 us
    pallas_call x4 -> x1, Pallas kernels: 174 us -> 197 us  [head_step(): pl.pallas_call(functools.partial(head_kernel, n, ways), out_shape=[jax.Sh...]
    dot_general x2 -> x0, matrix products: 17.5 us -> none  [local(): jnp.einsum('nsrd,nsrv->dv', rows, part, preferred_element_type=jnp.float32)]
    reduce_sum x9 -> x0, other arithmetic: 13.5 us -> none  [the longest x1 3.25 us: local(): label_part = jnp.sum(jnp.where(hitting, logits, 0.0), axis=-1)]
    convert_element_type x4 -> x0, other arithmetic: 7.38 us -> none  [the longest x1 2.85 us: local(): slopes = (factors[:, None, None] * row_weight[..., None] * (softmax - hit...]
    unnamed x0 -> x1, local copies, waits for them, and re-layouts: none -> 4.64 us
    reduce_max x2 -> x0, other arithmetic: 3.48 us -> none  [the longest x1 2.54 us: local(): local_top = jnp.max(logits, axis=-1)]
  transfers between devices with their start and end apart: 1 -> 0, of which waited for: 0 -> 0; matrix products, arithmetic and copies ran while one was open for 5% -> 0% of each run, Pallas kernels for 20% -> 0%
where the time goes in v1:
time: 205 us
  Pallas kernels  197 us (96%)
  local copies, waits for them, and re-layouts  7.12 us (3%)
    pallas_call x1, Pallas kernels, head_step(): pl.pallas_call(functools.partial(head_kernel, n, ways), out_shape=[jax.Sh...  197 us
    unnamed x1, local copies, waits for them, and re-layouts  4.64 us

profile of v1, /device:TPU:0, one launch (start us, length us, event | category | flops | bytes accessed | tf_op | source)
XLA Modules:
  0.0 205.1 jit_solution(12695433016179566266)
XLA Ops:
  0.6 1.3 broadcast_in_dim.9.gain
  1.9 197.4 %head_step.1 = (f32[2048,512]{1,0:T(8,128)}, f32[8,128]{1,0:T(8,128)}) custom-call(bf16[2,128,2048]{2,1,0:T(8,128)(2,1)} %x_in.1, bf16[1,2048]{1,0:T(2,128)(2,1)} %broadcast_in_dim.9.gain, bf16[2048,512]{1,0:T(8,128)(2,1)} %w_in.1, s32[1,128]{1,0:T(1,128)} %bitcast.3, s32[1,128]{1,0:T(1,128)} %bitcast.4, s32[2]{0:T(128)} %offsets.1), custom_call_target="tpu_custom_call" | custom-call | tf_op jit(solution)/shard_map/head_step/pallas_call | solution.py:570
  199.3 1.2 slice.3
  200.5 4.6 %copy.9 = f32[2048,512]{1,0:T(8,128)} copy(f32[2048,512]{1,0:T(8,128)} %get-tuple-element.9) | data formatting | bytes 8388608

commit v2 on v1

--- a/solution.py
+++ b/solution.py
@@ -15,9 +15,14 @@
 step_decay = 0.8
 MESH = pl.DeviceIdType.MESH
 
-PACE = 2
-LAG = 1
-EARLY = 3
+SPLIT = 2
+GAP = 3
+SPACE = 3
+UNIT = 1
+LAG = 3
+OWN = 6
+EARLY = 1
+HOLD = 18
 
 
 def rows_to_columns(row):
@@ -25,21 +30,22 @@
 
 
 def head_kernel(
-    n, ways, x_in, gain, w_in, labels, mask, offsets, grad, loss,
-    xv, held, wall, logits, s_own, s_got, labcol, wcol, lcol, tok, statall, lserow, labpart, num,
+    n, ways, x_in, gain, w_in, labels, mask, offsets, grad_out, loss,
+    grad, xv, held, wall, logits, s_own, s_got, labcol, wcol, lcol, tok, statall, lserow, labpart, num,
     count, sqall, invcol, lossall,
     send, recv, xsend, wsend, wrecv, sqsend, sqrecv, ssend, srecv, tsend, trecv, gsend, grecv,
-    lsend, lrecv, local_sem,
+    lsend, lrecv, local_sem, out_sem,
 ):
     steps, rows, width = xv.shape
     vocab = w_in.shape[1]
-    pieces = held.shape[0]
+    pieces, few = held.shape[0], held.shape[2]
     each = rows // ways
+    split = each // few
+    chunks = steps * split
     line = n // 4
-    total_rows = n * each
-    groups = total_rows // LANES
-    main = steps * ways
-    per_step = PACE * ways
+    chunk_rows = n * few
+    groups = chunk_rows // LANES
+    main = chunks * ways
     me, rank = lax.axis_index("dp"), lax.axis_index("tensor")
     c, x, z = lax.rem(me, 2), lax.rem(me // 2, 2), me // 4
     sibling, other = 1 - c, 1 - x
@@ -47,6 +53,9 @@
 
     def at(z_, x_, c_):
         return (z_ * 2 + x_) * 2 + c_
+
+    def first(q, p):
+        return q * ways + p
 
     def second(q, far):
         return main + q * (ways - 1) + far - 1
@@ -97,7 +106,7 @@
         )
 
     def x_copy(q, far):
-        target = q * ways + ways - far
+        target = first(q, ways - far)
         return to_tensor(
             held.at[second(q, far), me],
             held.at[target, me],
@@ -185,7 +194,7 @@
     labpart[...] = jnp.zeros_like(labpart)
     num[...] = jnp.zeros_like(num)
     count[...] = jnp.zeros_like(count)
-    statall[:, me] = jnp.zeros((steps, 2, 8, LANES), f32)
+    statall[:, me] = jnp.zeros((chunks, 2, 8, LANES), f32)
     for far in range(1, ways):
         square_copy(far).wait_recv()
     for s in range(steps):
@@ -199,26 +208,29 @@
         for far in range(ways):
             owner = lax.rem(rank + far, ways)
             offset = pl.multiple_of(owner * each, each)
-            i = second(s, far) if far else s * ways
-            scale = invcol[s, pl.ds(offset, each)]
-
-            def normalise(j, carry, s=s, i=i, offset=offset, scale=scale):
-                at_lane = pl.ds(pl.multiple_of(j * LANES, LANES), LANES)
+            scale = jnp.concatenate([invcol[s, pl.ds(offset, each)]] * 2, axis=1)
+
+            def normalise(j, carry, s=s, far=far, offset=offset, scale=scale):
+                at_lane = pl.ds(pl.multiple_of(j * 2 * LANES, 2 * LANES), 2 * LANES)
                 wide = xv[s, pl.ds(offset, each), at_lane].astype(f32)
-                held[i, me, :, at_lane] = (wide * scale * gain[:, at_lane].astype(f32)).astype(
-                    jnp.bfloat16
-                )
+                value = (wide * scale * gain[at_lane].astype(f32)[None]).astype(jnp.bfloat16)
+                for sub in range(split):
+                    q = s * split + sub
+                    i = second(q, far) if far else first(q, 0)
+                    held[i, me, :, at_lane] = value[sub * few : (sub + 1) * few]
                 return carry
 
-            lax.fori_loop(0, width // LANES, normalise, 0)
-    for s in range(steps):
+            lax.fori_loop(0, width // (2 * LANES), normalise, 0)
+    for q in range(chunks):
         for far in range(1, ways):
-            x_copy(s, far).start()
+            x_copy(q, far).start()
     for far in range(1, ways):
         w_copy(far).start()
 
-    def relay(i, k):
-        valid = jnp.logical_and(jnp.logical_and(i >= 0, i < pieces), k <= line)
+    def relay(k, t):
+        j = lax.rem(t, GAP * ways)
+        i = ways * (t // (GAP * ways)) + j
+        valid = jnp.logical_and(jnp.logical_and(t >= 0, j < ways), i < pieces)
         early = lax.rem(i, 6) == EARLY
         foreign = jnp.logical_and(i < main, lax.rem(i, ways) > 0)
 
@@ -265,6 +277,43 @@
                     along(zz, b)
 
                 beside(i, b).start()
+
+    def drain(i, carry):
+        early = lax.rem(i, 6) == EARLY
+
+        def one(zz, carry):
+            own, far_side = at(zz, x, c), at(zz, other, c)
+            up = jnp.logical_and(zz <= z, z < line - 1)
+            down = jnp.logical_and(zz >= z, z > 0)
+            beside(i, own).wait_send()
+            beside(i, far_side).wait_send()
+
+            @pl.when(up)
+            def _():
+                ups(i, own).wait_send()
+
+            @pl.when(down)
+            def _():
+                downs(i, own).wait_send()
+
+            @pl.when(jnp.logical_or(zz == z, jnp.logical_not(early)))
+            def _():
+                across(i, own).wait_send()
+
+            @pl.when(early)
+            def _():
+                @pl.when(up)
+                def _():
+                    ups(i, far_side).wait_send()
+
+                @pl.when(down)
+                def _():
+                    downs(i, far_side).wait_send()
+
+            return carry
+
+        lax.fori_loop(0, line, one, 0)
+        return carry
 
     def token_block(b):
         here = tok[b].astype(f32)
@@ -289,43 +338,42 @@
             labcol[s, span] = rows_to_columns(chosen[0:1])
             wcol[s, span] = rows_to_columns(weight)
 
-    def own_span(b):
-        return pl.ds(pl.multiple_of(b * rows + rank * each, each), each)
-
-    def hits(s, b, chunk):
+    def tokens(q, b):
+        start = b * rows + rank * each + lax.rem(q, split) * few
+        return q // split, pl.ds(pl.multiple_of(start, few), few)
+
+    def hits(q, b, chunk):
         columns = (
-            me * vocab + chunk * LANES + lax.broadcasted_iota(jnp.int32, (each, LANES), 1)
+            me * vocab + chunk * LANES + lax.broadcasted_iota(jnp.int32, (few, LANES), 1)
         ).astype(f32)
-        return labcol[s, own_span(b)] == columns
+        return labcol[tokens(q, b)] == columns
 
     def folded(values):
-        return jnp.sum(values.reshape(each // 8, 8, LANES), axis=0)
+        return jnp.sum(values.reshape(few // 8, 8, LANES), axis=0)
 
     def logits_unit(q, zz):
-        for core_x in range(2):
-            for p in range(ways):
-                b = at(zz, core_x, sibling)
-                beside(q * ways + p, b).wait_recv()
         acc = None
         for p in range(ways):
-            lhs = held[q * ways + p, pl.ds(4 * zz, 4)].reshape(4 * each, width)
+            for core_x in range(2):
+                beside(first(q, p), at(zz, core_x, sibling)).wait_recv()
+        for p in range(ways):
+            lhs = held[first(q, p), pl.ds(4 * zz, 4)].reshape(4 * few, width)
             part = jnp.dot(lhs, wall[p], preferred_element_type=f32)
             acc = part if acc is None else acc + part
-        span = pl.ds(pl.multiple_of(zz * 4 * each, 4 * each), 4 * each)
-        logits[q, span] = acc
+        logits[q, pl.ds(4 * zz, 4)] = acc.reshape(4, few, vocab)
 
         def block_stats(j, carry):
             b = 4 * zz + j
-            span = pl.ds(pl.multiple_of(b * each, each), each)
-            tile = logits[q, span]
+            span = pl.ds(pl.multiple_of(b * few, few), few)
+            tile = logits[q, b]
             top = jnp.max(tile, axis=1, keepdims=True)
             lse = top + jnp.log(jnp.sum(jnp.exp(tile - top), axis=1, keepdims=True))
-            lcol[q, span] = jnp.broadcast_to(lse, (each, LANES))
-            found = jnp.zeros((each, LANES), f32)
+            lcol[q, span] = jnp.broadcast_to(lse, (few, LANES))
+            found = jnp.zeros((few, LANES), f32)
             for chunk in range(vocab // LANES):
                 part = tile[:, chunk * LANES : (chunk + 1) * LANES]
                 found = found + jnp.where(hits(q, b, chunk), part, 0.0)
-            labpart[q] = labpart[q] + folded(wcol[q, own_span(b)] * found)
+            labpart[q] = labpart[q] + folded(wcol[tokens(q, b)] * found)
             return carry
 
         lax.fori_loop(0, 4, block_stats, 0)
@@ -366,18 +414,18 @@
         lax.fori_loop(0, groups, group, 0)
         factor = jnp.float32(1.0)
         for s in range(1, steps):
-            factor = jnp.where(q == s, jnp.float32(step_decay**s), factor)
+            factor = jnp.where(q // split == s, jnp.float32(step_decay**s), factor)
 
         def block(b, carry):
-            span = pl.ds(pl.multiple_of(b * each, each), each)
+            span = pl.ds(pl.multiple_of(b * few, few), few)
             lse = lcol[q, span]
-            weight = wcol[q, own_span(b)]
+            weight = wcol[tokens(q, b)]
             scale = factor * weight
             for chunk in range(vocab // LANES):
                 lanes = pl.ds(chunk * LANES, LANES)
-                softmax = jnp.exp(logits[q, span, lanes] - lse)
+                softmax = jnp.exp(logits[q, b, :, lanes] - lse)
                 hit = jnp.where(hits(q, b, chunk), 1.0, 0.0)
-                s_own[q, span, lanes] = (scale * (softmax - hit)).astype(jnp.bfloat16)
+                s_own[q, b, :, lanes] = (scale * (softmax - hit)).astype(jnp.bfloat16)
             return carry + folded(weight * lse)
 
         weighted = lax.fori_loop(0, n, block, zero)
@@ -388,171 +436,171 @@
         )
         num[q] = jnp.broadcast_to(numerator, (8, LANES))
 
-    def add_gradient(i, slopes, first):
-        block = 256 if width % 256 == 0 else LANES
+    block = 256 if width % 256 == 0 else LANES
+    blocks = width // block
+
+    def out_copy(j):
+        lanes = pl.ds(pl.multiple_of(j * block, block), block)
+        return pltpu.make_async_copy(grad.at[lanes], grad_out.at[lanes], out_sem.at[j])
+
+    def add_gradient(i, slopes, first_time, last_time):
 
         def part(j, carry):
             lanes = pl.ds(pl.multiple_of(j * block, block), block)
-            lhs = held[i, :, :, lanes].reshape(total_rows, block)
+            lhs = held[i, :, :, lanes].reshape(chunk_rows, block)
+            rhs = slopes[...].reshape(chunk_rows, vocab)
             value = lax.dot_general(
-                lhs, slopes[...], (((0,), (0,)), ((), ())), preferred_element_type=f32
+                lhs, rhs, (((0,), (0,)), ((), ())), preferred_element_type=f32
             )
 
-            @pl.when(first)
+            @pl.when(first_time)
             def _():
                 grad[lanes, :] = value
 
-            @pl.when(jnp.logical_not(first))
+            @pl.when(jnp.logical_not(first_time))
             def _():
                 grad[lanes, :] = grad[lanes, :] + value
 
+            @pl.when(jnp.logical_and(last_time, j > 0))
+            def _():
+                out_copy(j - 1).start()
+
             return carry
 
-        lax.fori_loop(0, width // block, part, 0)
-
-    base = PACE * (ways - 1) + 2
-    slopes_base = base + line - 1 + LAG
-    got_base = PACE * (main + ways - 2) + line + 1
-    got_pace = PACE * (ways - 1)
-    depth = line // PACE + 1
-
-    def wave(w, carry):
-        for d in range(depth - 1, -1, -1):
-            i = w // PACE - d
-            relay(i, w - PACE * i)
-
-        @pl.when(jnp.logical_and(w >= 1, w <= line))
+        lax.fori_loop(0, blocks, part, 0)
+
+    def larger(a, b):
+        both = isinstance(a, int) and isinstance(b, int)
+        return max(a, b) if both else jnp.maximum(a, b)
+
+    def ready(i, k):
+        return GAP * ways * (i // ways) + i % ways + SPACE * k
+
+    def unit_slot(q, u):
+        held_back = HOLD + q * line + u - 1000 * (q // split)
+        return larger(ready(q * ways + ways - 1, u + 1) + UNIT, larger(held_back, HOLD))
+
+    def slopes_slot(q):
+        return unit_slot(q, line - 1) + LAG
+
+    def got_slot(q):
+        return larger(ready(second(q, ways - 1), line), slopes_slot(q)) + 1
+
+    final = chunks - 1
+    slots = 1 + max(ready(pieces - 1, line), slopes_slot(final) + OWN, got_slot(final))
+    assert slopes_slot(0) + OWN < got_slot(0) and slopes_slot(final) + OWN < got_slot(final)
+    assert all(unit_slot(q, 0) >= unit_slot(0, 0) for q in range(chunks))
+    drained = sum(ready(i, line + 2) < slots for i in range(pieces))
+
+    def slot(w, carry):
+        for k in range(line, -1, -1):
+            relay(k, w - SPACE * k)
+        t = w - SPACE * (line + 2)
+        i = ways * (t // (GAP * ways)) + lax.rem(t, GAP * ways)
+
+        @pl.when(jnp.logical_and(t >= 0, jnp.logical_and(lax.rem(t, GAP * ways) < ways, i < drained)))
+        def _():
+            drain(i, 0)
+
+        @pl.when(jnp.logical_and(w >= 1, w <= n))
         def _():
             @pl.when(w == 1)
             def _():
                 for j in range(1, n):
                     token_wait(j).wait_recv()
 
-            def one(j, carry):
-                token_block(4 * (w - 1) + j)
-                return carry
-
-            lax.fori_loop(0, 4, one, 0)
-
-        @pl.when(w == base)
+            token_block(w - 1)
+
+        @pl.when(w == unit_slot(0, 0))
         def _():
             w_load.wait()
             for far in range(1, ways):
                 w_copy(far).wait_recv()
 
-        t = w - base
-        q, u = t // per_step, lax.rem(t, per_step)
-        active = jnp.logical_and(t >= 0, jnp.logical_and(q < steps, u < line))
-
-        @pl.when(active)
-        def _():
-            def one(side, carry):
-                zz = z + u * (2 * side - 1)
-
-                @pl.when(jnp.logical_and(inside(zz), u >= side))
+        def chunk(q, carry):
+            @pl.when(jnp.logical_and(w >= unit_slot(q, 0), w <= unit_slot(q, line - 1)))
+            def _():
+                def unit(v, carry):
+                    u, side = v // 2, lax.rem(v, 2)
+                    zz = z + u * (2 * side - 1)
+                    now = jnp.logical_and(w == unit_slot(q, u), u >= side)
+
+                    @pl.when(jnp.logical_and(now, inside(zz)))
+                    def _():
+                        logits_unit(q, zz)
+
+                    return carry
+
+                lax.fori_loop(0, 2 * line, unit, 0)
+
+                @pl.when(w == unit_slot(q, line - 1))
                 def _():
-                    logits_unit(q, zz)
-
-                return carry
-
-            lax.fori_loop(0, 2, one, 0)
-
-            @pl.when(u == line - 1)
-            def _():
-                send_stats(q)
-
-        ts = w - slopes_base
-        qs = ts // per_step
-
-        @pl.when(jnp.logical_and(jnp.logical_and(ts >= 0, lax.rem(ts, per_step) == 0), qs < steps))
-        def _():
-            make_slopes(qs)
-
-            @pl.when(qs == steps - 1)
-            def _():
-                lossall[0] = num[...]
+                    send_stats(q)
+
+            @pl.when(w == slopes_slot(q))
+            def _():
+                make_slopes(q)
+
+                @pl.when(q == chunks - 1)
+                def _():
+                    lossall[0] = num[...]
+                    for far in range(1, ways):
+                        loss_copy(far).start()
+
+            @pl.when(w == slopes_slot(q) + OWN)
+            def _():
+                add_gradient(first(q, 0), s_own.at[q], q == 0, False)
+
+            @pl.when(w == got_slot(q))
+            def _():
                 for far in range(1, ways):
-                    loss_copy(far).start()
-
-            add_gradient(qs * ways, s_own.at[qs], qs == 0)
-
-        tg = w - got_base
-        qg = tg // got_pace
-
-        @pl.when(jnp.logical_and(jnp.logical_and(tg >= 0, lax.rem(tg, got_pace) == 0), qg < steps))
-        def _():
-            for far in range(1, ways):
-                i = second(qg, far)
-                slope_copy(qg, ways - far).wait_recv()
-
-                def arrived(j, carry, i=i):
-                    beside(i, 2 * j + sibling).wait_recv()
-                    return carry
-
-                lax.fori_loop(0, 2 * line, arrived, 0)
-                add_gradient(i, s_got.at[far - 1, qg], False)
-
+                    i = second(q, far)
+                    slope_copy(q, ways - far).wait_recv()
+
+                    def arrived(j, carry, i=i):
+                        beside(i, 2 * j + sibling).wait_recv()
+                        return carry
+
+                    lax.fori_loop(0, 2 * line, arrived, 0)
+                    add_gradient(i, s_got.at[far - 1, q], False, jnp.logical_and(q == final, far == ways - 1))
+
+            return carry
+
+        lax.fori_loop(0, chunks, chunk, 0)
         return carry
 
-    waves = max(
-        PACE * (pieces - 1) + line + 1,
-        slopes_base + (steps - 1) * per_step + 1,
-        got_base + (steps - 1) * got_pace + 1,
-    )
-    lax.fori_loop(0, waves, wave, 0)
-
+    lax.fori_loop(0, slots, slot, 0)
+
+    out_copy(blocks - 1).start()
     for far in range(1, ways):
         loss_copy(far).wait_recv()
     result = jnp.zeros((8, LANES), f32)
     for s in range(steps):
-        numerator = lossall[0, s]
-        for p in range(1, ways):
-            numerator = numerator + lossall[p, s]
+        numerator = jnp.zeros((8, LANES), f32)
+        for p in range(ways):
+            for sub in range(split):
+                numerator = numerator + lossall[p, s * split + sub]
         counted = jnp.sum(
             jnp.sum(count[s], axis=0, keepdims=True), axis=1, keepdims=True
         )
         result = result + step_decay**s * numerator / jnp.broadcast_to(counted, (8, LANES))
-    loss[...] = result
-
-    def finish(u, carry):
-        i, b = u // n, lax.rem(u, n)
-        early = lax.rem(i, 6) == EARLY
-        cb, xb, zb = lax.rem(b, 2), lax.rem(b // 2, 2), b // 4
-        mine = cb == c
-        column = jnp.logical_and(mine, xb == x)
-        lined = jnp.logical_and(mine, jnp.logical_or(xb == x, early))
-
-        @pl.when(jnp.logical_and(lined, jnp.logical_and(zb <= z, z < line - 1)))
-        def _():
-            ups(i, b).wait_send()
-
-        @pl.when(jnp.logical_and(lined, jnp.logical_and(zb >= z, z > 0)))
-        def _():
-            downs(i, b).wait_send()
-
-        @pl.when(jnp.logical_and(column, jnp.logical_or(zb == z, jnp.logical_not(early))))
-        def _():
-            across(i, b).wait_send()
-
-        @pl.when(mine)
-        def _():
-            beside(i, b).wait_send()
-
-        return carry
-
-    lax.fori_loop(0, pieces * n, finish, 0)
+    loss[...] = result[0:1, 0:1]
+
+    lax.fori_loop(drained, pieces, drain, 0)
+    for j in range(blocks):
+        out_copy(j).wait()
     for j in range(1, n):
         token_copy(j).wait_send()
     for far in range(1, ways):
         square_copy(far).wait_send()
         w_copy(far).wait_send()
         loss_copy(far).wait_send()
-    for s in range(steps):
+    for q in range(chunks):
         for j in range(1, n):
-            stat_copy(s, j).wait_send()
+            stat_copy(q, j).wait_send()
         for far in range(1, ways):
-            x_copy(s, far).wait_send()
-            slope_copy(s, far).wait_send()
+            x_copy(q, far).wait_send()
+            slope_copy(q, far).wait_send()
 
 
 def head_step(hidden, gain, weight, labels, mask, offsets):
@@ -560,8 +608,10 @@
     vocab = weight.shape[1]
     n, ways = lax.axis_size("dp"), lax.axis_size("tensor")
     each = rows // ways
-    total_rows = n * each
-    pieces = steps * (2 * ways - 1)
+    split = SPLIT if each % (16 * SPLIT) == 0 else 1
+    few = each // split
+    chunks = steps * split
+    pieces = chunks * (2 * ways - 1)
     vmem = pl.BlockSpec(memory_space=pltpu.VMEM)
     smem = pl.BlockSpec(memory_space=pltpu.SMEM)
     hbm = pl.BlockSpec(memory_space=pl.ANY)
@@ -571,45 +621,47 @@
         functools.partial(head_kernel, n, ways),
         out_shape=[
             jax.ShapeDtypeStruct((width, vocab), f32),
-            jax.ShapeDtypeStruct((8, LANES), f32),
+            jax.ShapeDtypeStruct((1, 1), f32),
         ],
         in_specs=[hbm, vmem, hbm, vmem, vmem, smem],
-        out_specs=[vmem, vmem],
+        out_specs=[hbm, vmem],
         scratch_shapes=[
+            pltpu.VMEM((width, vocab), f32),
             pltpu.VMEM((steps, rows, width), bf16),
-            pltpu.VMEM((pieces, n, each, width), bf16),
+            pltpu.VMEM((pieces, n, few, width), bf16),
             pltpu.VMEM((ways, width, vocab), bf16),
-            pltpu.VMEM((steps, total_rows, vocab), f32),
-            pltpu.VMEM((steps, total_rows, vocab), bf16),
-            pltpu.VMEM((ways - 1, steps, total_rows, vocab), bf16),
+            pltpu.VMEM((chunks, n, few, vocab), f32),
+            pltpu.VMEM((chunks, n, few, vocab), bf16),
+            pltpu.VMEM((ways - 1, chunks, n, few, vocab), bf16),
             pltpu.VMEM((steps, n * rows, LANES), f32),
             pltpu.VMEM((steps, n * rows, LANES), f32),
-            pltpu.VMEM((steps, total_rows, LANES), f32),
+            pltpu.VMEM((chunks, n * few, LANES), f32),
             pltpu.VMEM((n, 8, rows), jnp.int32),
-            pltpu.VMEM((steps, n, 2, 8, LANES), f32),
-            pltpu.VMEM((steps, 8, LANES), f32),
-            pltpu.VMEM((steps, 8, LANES), f32),
-            pltpu.VMEM((steps, 8, LANES), f32),
+            pltpu.VMEM((chunks, n, 2, 8, LANES), f32),
+            pltpu.VMEM((chunks, 8, LANES), f32),
+            pltpu.VMEM((chunks, 8, LANES), f32),
+            pltpu.VMEM((chunks, 8, LANES), f32),
             pltpu.VMEM((steps, 8, rows), f32),
             pltpu.VMEM((ways, steps, 8, rows), f32),
             pltpu.VMEM((steps, rows, LANES), f32),
-            pltpu.VMEM((ways, steps, 8, LANES), f32),
+            pltpu.VMEM((ways, chunks, 8, LANES), f32),
             dma((4, pieces, n // 2)),
             dma((pieces, n)),
-            dma((steps, ways - 1)),
+            dma((chunks, ways - 1)),
             dma((ways - 1,)),
             dma((ways - 1,)),
             dma((ways - 1,)),
             dma((ways - 1,)),
-            dma((steps, n)),
-            dma((steps, n)),
+            dma((chunks, n)),
+            dma((chunks, n)),
             dma((n,)),
             dma((n,)),
-            dma((ways - 1, steps)),
-            dma((ways - 1, steps)),
+            dma((ways - 1, chunks)),
+            dma((ways - 1, chunks)),
             dma((ways - 1,)),
             dma((ways - 1,)),
             dma((2,)),
+            dma((width // LANES,)),
         ],
         compiler_params=pltpu.CompilerParams(
             collective_id=7, has_side_effects=True, vmem_limit_bytes=60 * 1024 * 1024
@@ -620,7 +672,7 @@
 
 def local(drafter_hidden, norm_gain, head_weight, labels, loss_mask, offsets):
     gradient, loss = head_step(
-        drafter_hidden, norm_gain[None], head_weight, labels[None], loss_mask[None], offsets
+        drafter_hidden, norm_gain, head_weight, labels[None], loss_mask[None], offsets
     )
     return (loss[0, 0], gradient)
 

time: 205 us -> 177 us (0.86)
  Pallas kernels: 197 us -> 170 us
  local copies, waits for them, and re-layouts: 7.12 us -> 4.64 us
    pallas_call x1, Pallas kernels: 197 us -> 170 us  [head_step(): pl.pallas_call(functools.partial(head_kernel, n, ways), out_shape=[jax.Sh...]
where the time goes in v2:
time: 177 us
  Pallas kernels  170 us (96%)
  local copies, waits for them, and re-layouts  4.64 us (3%)
  between operations  2.37 us (1%)
    pallas_call x1, Pallas kernels, head_step(): pl.pallas_call(functools.partial(head_kernel, n, ways), out_shape=[jax.Sh...  170 us
    unnamed x1, local copies, waits for them, and re-layouts  4.64 us

profile of v2, /device:TPU:0, one launch (start us, length us, event | category | flops | bytes accessed | tf_op | source)
XLA Modules:
  0.0 176.6 jit_solution(13195873867994644359)
XLA Ops:
  0.6 169.6 %head_step.1 = (f32[2048,512]{1,0:T(8,128)}, f32[1,1]{1,0:T(1,128)}) custom-call(bf16[2,128,2048]{2,1,0:T(8,128)(2,1)} %x_in.1, bf16[2048]{0:T(1024)(128)(2,1)} %gain.1, bf16[2048,512]{1,0:T(8,128)(2,1)} %w_in.1, s32[1,128]{1,0:T(1,128)} %bitcast.3, s32[1,128]{1,0:T(1,128)} %bitcast.4, s32[2]{0:T(128)} %offsets.1), custom_call_target="tpu_custom_call" | custom-call | tf_op jit(solution)/shard_map/head_step/pallas_call | solution.py:620
  170.9 4.6 %copy.11 = f32[2048,512]{1,0:T(8,128)} copy(f32[2048,512]{1,0:T(8,128)} %get-tuple-element.9) | data formatting | bytes 8388608

commit v3 on v2

--- a/solution.py
+++ b/solution.py
@@ -436,7 +436,7 @@
         )
         num[q] = jnp.broadcast_to(numerator, (8, LANES))
 
-    block = 256 if width % 256 == 0 else LANES
+    block = 512 if width % 512 == 0 else LANES
     blocks = width // block
 
     def out_copy(j):

time: 177 us -> 174 us (0.983)
  Pallas kernels: 170 us -> 167 us
    pallas_call x1, Pallas kernels: 170 us -> 167 us  [head_step(): pl.pallas_call(functools.partial(head_kernel, n, ways), out_shape=[jax.Sh...]
where the time goes in v3:
time: 174 us
  Pallas kernels  167 us (96%)
  local copies, waits for them, and re-layouts  4.64 us (3%)
  between operations  2.37 us (1%)
    pallas_call x1, Pallas kernels, head_step(): pl.pallas_call(functools.partial(head_kernel, n, ways), out_shape=[jax.Sh...  167 us
    unnamed x1, local copies, waits for them, and re-layouts  4.64 us

profile of v3, /device:TPU:0, one launch (start us, length us, event | category | flops | bytes accessed | tf_op | source)
XLA Modules:
  0.0 173.8 jit_solution(8846263822703000828)
XLA Ops:
  0.6 166.8 %head_step.1 = (f32[2048,512]{1,0:T(8,128)}, f32[1,1]{1,0:T(1,128)}) custom-call(bf16[2,128,2048]{2,1,0:T(8,128)(2,1)} %x_in.1, bf16[2048]{0:T(1024)(128)(2,1)} %gain.1, bf16[2048,512]{1,0:T(8,128)(2,1)} %w_in.1, s32[1,128]{1,0:T(1,128)} %bitcast.3, s32[1,128]{1,0:T(1,128)} %bitcast.4, s32[2]{0:T(128)} %offsets.1), custom_call_target="tpu_custom_call" | custom-call | tf_op jit(solution)/shard_map/head_step/pallas_call | solution.py:620
  168.0 4.6 %copy.11 = f32[2048,512]{1,0:T(8,128)} copy(f32[2048,512]{1,0:T(8,128)} %get-tuple-element.9) | data formatting | bytes 8388608

commit v4 on v3

--- a/solution.py
+++ b/solution.py
@@ -19,8 +19,8 @@
 GAP = 3
 SPACE = 3
 UNIT = 1
-LAG = 3
-OWN = 6
+LAG = 4
+OWN = 5
 EARLY = 1
 HOLD = 18
 

time: 174 us -> 172 us (0.989)
  Pallas kernels: 167 us -> 165 us
    pallas_call x1, Pallas kernels: 167 us -> 165 us  [head_step(): pl.pallas_call(functools.partial(head_kernel, n, ways), out_shape=[jax.Sh...]
where the time goes in v4:
time: 172 us
  Pallas kernels  165 us (96%)
  local copies, waits for them, and re-layouts  4.64 us (3%)
  between operations  2.37 us (1%)
    pallas_call x1, Pallas kernels, head_step(): pl.pallas_call(functools.partial(head_kernel, n, ways), out_shape=[jax.Sh...  165 us
    unnamed x1, local copies, waits for them, and re-layouts  4.64 us

profile of v4, /device:TPU:0, one launch (start us, length us, event | category | flops | bytes accessed | tf_op | source)
XLA Modules:
  0.0 171.8 jit_solution(2961089297087927673)
XLA Ops:
  0.6 164.8 %head_step.1 = (f32[2048,512]{1,0:T(8,128)}, f32[1,1]{1,0:T(1,128)}) custom-call(bf16[2,128,2048]{2,1,0:T(8,128)(2,1)} %x_in.1, bf16[2048]{0:T(1024)(128)(2,1)} %gain.1, bf16[2048,512]{1,0:T(8,128)(2,1)} %w_in.1, s32[1,128]{1,0:T(1,128)} %bitcast.3, s32[1,128]{1,0:T(1,128)} %bitcast.4, s32[2]{0:T(128)} %offsets.1), custom_call_target="tpu_custom_call" | custom-call | tf_op jit(solution)/shard_map/head_step/pallas_call | solution.py:620
  166.0 4.6 %copy.11 = f32[2048,512]{1,0:T(8,128)} copy(f32[2048,512]{1,0:T(8,128)} %get-tuple-element.9) | data formatting | bytes 8388608
